TPU v7x, 32 devices: a 4x2x2 block of a 4x4x8 slice. The times are simulated.
32 devices in a mesh: dp: 4 (over y, z), sp: 8 (over x, core).
Axes of the slice: x: 4, y: 2, z: 2, core: 2. Of those that a mesh axis runs over, the one named last changes fastest.
The devices are a block of a 4x4x8 slice.
Arguments:
- x_in: bfloat16 [32, 512, 1024], P('dp', 'sp'), parts along dimension 0
- grad_y: bfloat16 [32, 512, 1024], P('dp', 'sp'), parts along dimension 0
- positions: int32 [2048], P(('dp', 'sp')), parts along dimension 0
- w_q: bfloat16 [1024, 2048], replicated
- w_k: bfloat16 [1024, 1024], replicated
- w_v: bfloat16 [1024, 1024], replicated
- w_o: bfloat16 [2048, 1024], replicated
- w_gate: bfloat16 [1024, 3072], replicated
- w_up: bfloat16 [1024, 3072], replicated
- w_down: bfloat16 [3072, 1024], replicated
- norm_gain: float32 [1024], replicated
- q_norm: float32 [16, 128], replicated
- k_norm: float32 [8, 128], replicated
Outputs:
- output 1: bfloat16 [32, 512, 1024], P('dp', 'sp'), parts along dimension 0
- output 2: bfloat16 [32, 512, 1024], P('dp', 'sp'), parts along dimension 0
- output 3: bfloat16 [4096, 2048], P('dp'), parts along dimension 0
- output 4: bfloat16 [4096, 1024], P('dp'), parts along dimension 0
- output 5: bfloat16 [4096, 1024], P('dp'), parts along dimension 0
- output 6: bfloat16 [8192, 1024], P('dp'), parts along dimension 0
- output 7: bfloat16 [4096, 3072], P('dp'), parts along dimension 0
- output 8: bfloat16 [4096, 3072], P('dp'), parts along dimension 0
- output 9: bfloat16 [12288, 1024], P('dp'), parts along dimension 0
- output 10: float32 [4096], P('dp'), parts along dimension 0
- output 11: float32 [64, 128], P('dp'), parts along dimension 0
- output 12: float32 [32, 128], P('dp'), parts along dimension 0
There are 4 independent parts. A program takes and returns all parts, laid end to end along the dimension named above; an argument that names none is the same for every part.
All inputs are finite; a program needn't handle non-finite values.
Results may differ from a plain program's by a relative error of at most 0.02.
Values are sent between devices in bfloat16 or wider.
A program may use at most 768 MiB of HBM per device.

v0:
```python
import jax
import jax.numpy as jnp
from jax import lax
from jax.sharding import PartitionSpec as P

NORM_EPS = 1e-5
ROPE_THETA = 75.0e6


def input_norm(x_f32, norm_gain):
    row_mean = jnp.mean(x_f32, axis=-1, keepdims=True)
    centered = x_f32 - row_mean
    row_var = jnp.mean(centered * centered, axis=-1, keepdims=True)
    return (centered * lax.rsqrt(row_var + NORM_EPS) * norm_gain).astype(jnp.bfloat16)


def rope_tables(positions, head_dim):
    inv_freq = ROPE_THETA ** (-(jnp.arange(head_dim // 2, dtype=jnp.float32) * 2.0) / head_dim)
    angles = positions.astype(jnp.float32)[:, None] * inv_freq[None, :]
    return jnp.cos(angles), jnp.sin(angles)


def head_prepare(proj_in, norm_weight, cos_t, sin_t):
    proj_f32 = proj_in.astype(jnp.float32)
    row_mean = jnp.mean(proj_f32, axis=-1, keepdims=True)
    centered = proj_f32 - row_mean
    row_var = jnp.mean(centered * centered, axis=-1, keepdims=True)
    normed = centered * lax.rsqrt(row_var + NORM_EPS) * norm_weight
    pair_view = normed.reshape(normed.shape[:-1] + (normed.shape[-1] // 2, 2))
    even_part = pair_view[..., 0]
    odd_part = pair_view[..., 1]
    cos_rows = cos_t[:, None, :]
    sin_rows = sin_t[:, None, :]
    rotated = jnp.stack([even_part * cos_rows - odd_part * sin_rows, even_part * sin_rows + odd_part * cos_rows], axis=-1)
    return rotated.reshape(normed.shape).astype(jnp.bfloat16)


def swiglu(gate_pre, up_proj):
    return (jax.nn.silu(gate_pre) * up_proj).astype(jnp.bfloat16)


def attend(q_rot, k_rot, v_proj, q_start):
    score_scale = q_rot.shape[-1] ** -0.5
    scores = jnp.einsum('bqkgd,bskd->bkgqs', q_rot, k_rot, preferred_element_type=jnp.float32) * score_scale
    q_index = q_start + jnp.arange(q_rot.shape[1])
    k_index = jnp.arange(k_rot.shape[1])
    causal = q_index[:, None] >= k_index[None, :]
    attn_probs = jax.nn.softmax(jnp.where(causal, scores, -1e30), axis=-1).astype(jnp.bfloat16)
    attended = jnp.einsum('bkgqs,bskd->bqkgd', attn_probs, v_proj, preferred_element_type=jnp.float32)
    return attended.astype(jnp.bfloat16)


def times_transposed(lhs_mat, rhs_mat):
    return lax.dot_general(lhs_mat, rhs_mat, (((1,), (1,)), ((), ())), preferred_element_type=jnp.float32)


def grad_product(act_rows, grad_rows):
    return lax.dot_general(act_rows, grad_rows, (((0,), (0,)), ((), ())), preferred_element_type=jnp.float32)


def solution(mesh):
    group_devices = mesh.shape['sp']
    seq_spec = P('dp', 'sp', None)
    grad_spec = P('dp', None)

    def layer_step(x_in, grad_y, positions, w_q, w_k, w_v, w_o, w_gate, w_up, w_down, norm_gain, q_norm, k_norm):
        batch_rows, local_len, model_dim = x_in.shape
        num_heads, head_dim = q_norm.shape
        num_kv = k_norm.shape[0]
        kv_copies = max(group_devices // num_kv, 1)
        full_len = local_len * group_devices
        tokens = batch_rows * local_len
        x_f32 = x_in.astype(jnp.float32)
        normed, norm_back = jax.vjp(input_norm, x_f32, norm_gain)
        flat_norm = normed.reshape(tokens, model_dim)
        q_proj = jnp.dot(flat_norm, w_q, preferred_element_type=jnp.float32).astype(jnp.bfloat16)
        k_proj = jnp.dot(flat_norm, w_k, preferred_element_type=jnp.float32).astype(jnp.bfloat16)
        v_proj = jnp.dot(flat_norm, w_v, preferred_element_type=jnp.float32).astype(jnp.bfloat16)
        cos_t, sin_t = rope_tables(positions, head_dim)
        q_rot, q_back = jax.vjp(lambda proj_in, weight: head_prepare(proj_in, weight, cos_t, sin_t), q_proj.reshape(batch_rows, local_len, num_heads, head_dim), q_norm)
        k_rot, k_back = jax.vjp(lambda proj_in, weight: head_prepare(proj_in, weight, cos_t, sin_t), k_proj.reshape(batch_rows, local_len, num_kv, head_dim), k_norm)
        v_heads = v_proj.reshape(batch_rows, local_len, num_kv, head_dim)
        q_by_head = lax.all_to_all(q_rot, 'sp', 2, 1, tiled=True)
        k_by_head = lax.all_to_all(jnp.repeat(k_rot, kv_copies, axis=2), 'sp', 2, 1, tiled=True)
        v_by_head = lax.all_to_all(jnp.repeat(v_heads, kv_copies, axis=2), 'sp', 2, 1, tiled=True)
        local_q = q_by_head.shape[2]
        local_kv = k_by_head.shape[2]
        grouped_shape = (batch_rows, full_len, local_kv, local_q // local_kv, head_dim)
        attn_heads, attn_back = jax.vjp(lambda q_arg, k_arg, v_arg: attend(q_arg, k_arg, v_arg, 0), q_by_head.reshape(grouped_shape), k_by_head, v_by_head)
        attn_seq = lax.all_to_all(attn_heads.reshape(batch_rows, full_len, local_q, head_dim), 'sp', 1, 2, tiled=True)
        attn_flat = attn_seq.reshape(tokens, num_heads * head_dim)
        attn_out = jnp.dot(attn_flat, w_o, preferred_element_type=jnp.float32).astype(jnp.bfloat16)
        gate_pre = jnp.dot(flat_norm, w_gate, preferred_element_type=jnp.float32)
        up_proj = jnp.dot(flat_norm, w_up, preferred_element_type=jnp.float32)
        hidden, act_back = jax.vjp(swiglu, gate_pre, up_proj)
        mlp_out = jnp.dot(hidden, w_down, preferred_element_type=jnp.float32).astype(jnp.bfloat16)
        y_out = (x_f32 + attn_out.astype(jnp.float32).reshape(x_in.shape) + mlp_out.astype(jnp.float32).reshape(x_in.shape)).astype(jnp.bfloat16)

        grad_flat = grad_y.reshape(tokens, model_dim)
        d_hidden = times_transposed(grad_flat, w_down).astype(jnp.bfloat16)
        d_gate, d_up = act_back(d_hidden)
        d_gate = d_gate.astype(jnp.bfloat16)
        d_up = d_up.astype(jnp.bfloat16)
        d_attn = times_transposed(grad_flat, w_o).astype(jnp.bfloat16)
        d_attn_heads = lax.all_to_all(d_attn.reshape(batch_rows, local_len, num_heads, head_dim), 'sp', 2, 1, tiled=True)
        dq_heads, dk_heads, dv_heads = attn_back(d_attn_heads.reshape(grouped_shape))
        dq_rot = lax.all_to_all(dq_heads.reshape(batch_rows, full_len, local_q, head_dim), 'sp', 1, 2, tiled=True)
        dk_copies = lax.all_to_all(dk_heads, 'sp', 1, 2, tiled=True)
        dv_copies = lax.all_to_all(dv_heads, 'sp', 1, 2, tiled=True)
        copy_shape = (batch_rows, local_len, num_kv, kv_copies, head_dim)
        dk_rot = jnp.sum(dk_copies.reshape(copy_shape), axis=3, dtype=jnp.float32).astype(jnp.bfloat16)
        dv_seq = jnp.sum(dv_copies.reshape(copy_shape), axis=3, dtype=jnp.float32).astype(jnp.bfloat16)
        dq_proj, grad_q_norm = q_back(dq_rot)
        dk_proj, grad_k_norm = k_back(dk_rot)
        dq_flat = dq_proj.reshape(tokens, num_heads * head_dim)
        dk_flat = dk_proj.reshape(tokens, num_kv * head_dim)
        dv_flat = dv_seq.reshape(tokens, num_kv * head_dim)
        d_norm = (times_transposed(dq_flat, w_q) + times_transposed(dk_flat, w_k) + times_transposed(dv_flat, w_v)
                  + times_transposed(d_gate, w_gate) + times_transposed(d_up, w_up)).astype(jnp.bfloat16)
        dx_norm, grad_gain = norm_back(d_norm.reshape(x_in.shape))
        grad_x = (grad_y.astype(jnp.float32) + dx_norm).astype(jnp.bfloat16)
        partial_mats = (grad_product(flat_norm, dq_flat), grad_product(flat_norm, dk_flat), grad_product(flat_norm, dv_flat),
                        grad_product(attn_flat, grad_flat), grad_product(flat_norm, d_gate), grad_product(flat_norm, d_up),
                        grad_product(hidden, grad_flat))
        summed_mats = [lax.psum(part_grad, 'sp').astype(jnp.bfloat16) for part_grad in partial_mats]
        summed_small = [lax.psum(part_grad, 'sp') for part_grad in (grad_gain, grad_q_norm, grad_k_norm)]
        return tuple([y_out, grad_x] + summed_mats + summed_small)

    in_specs = (seq_spec, seq_spec, P(('dp', 'sp'))) + (P(),) * 10
    out_specs = (seq_spec, seq_spec) + (grad_spec,) * 7 + (P('dp'), grad_spec, grad_spec)
    return jax.shard_map(layer_step, mesh=mesh, in_specs=in_specs, out_specs=out_specs, check_vma=False)
```

profile of v0, /device:TPU:81, one launch (start us, length us, event | category | flops | bytes accessed | tf_op | source)
XLA Modules:
  0.0 1150.1 jit_solution(1935714444415679753)
XLA Ops:
  38.4 6.5 all-to-all-start.1
  45.0 8.2 fusion.88
  53.1 7.8 convolution_convert_fusion.1
  74.3 7.0 reshape.391
  88.0 7.8 copy.332
  106.1 12.7 %fusion.18 = (bf16[512,3072]{1,0:T(8,128)(2,1)}, bf16[512,3072]{1,0:T(8,128)(2,1)}, f32[512,3072]{1,0:T(8,128)}) fusion(f32[512,3072]{1,0:T(8,128)} %fusion.88, bf16[512,3072]{1,0:T(8,128)(2,1)S(1)} %copy-done.86, bf16[512,1024]{1,0:T(8,128)(2,1)S(1)} %bitcast.337, bf16[1024,3072]{1,0:T(8,128)(2,1)} %param.20), kind=kOutput, calls=%fused_computation.33 | convolution fusion | flops 3244818432 | bytes 29360128 | tf_op jit(solution)/shard_map/dot_general | solution.py:93
  131.8 6.7 subtract_convert_fusion
  154.1 8.3 fusion.95
  167.2 11.0 fusion.85
  178.2 6.4 fusion.96
  184.7 8.6 all-to-all-done.4
  199.0 8.6 fusion.91
  207.6 7.2 convolution_convert_fusion.6
  227.3 7.3 fusion.9
  234.6 9.2 fusion.73
  243.9 9.9 fusion.61
  253.8 9.0 fusion.8
  262.9 12.6 %fusion.46 = bf16[8,512,2,128]{3,1,2,0:T(8,128)(2,1)} fusion(bf16[8,512,128,1]{2,1,3,0:T(8,128)(2,1)S(1)} %bitcast.333, bf16[8,2,512,512]{2,3,1,0:T(8,128)(2,1)S(1)} %get-tuple-element.118, f32[8,2,512]{2,1,0:T(2,128)S(1)} %neg.37, f32[8,2,512]{2,1,0:T(2,128)S(1)} %fusion.73, pred[512,512]{0,1:T(8,128)(4,1)S(1)} %iota_compare_fusion, ...), kind=kOutput, calls=%fused_computation.99 | convolution fusion | flops 1112539136 | bytes 28672000 | tf_op jit(solution)/shard_map/transpose(jvp(bqkgd,bskd->bkgqs))/dot_general | solution.py:44
  275.4 11.8 %fusion.57 = bf16[8,512,1,128]{3,1,0,2:T(8,128)(2,1)S(1)} fusion(bf16[8,512,2,128]{3,1,2,0:T(8,128)(2,1)S(1)} %bitcast.322, bf16[8,2,512,512]{2,3,1,0:T(8,128)(2,1)S(1)} %get-tuple-element.118, f32[8,2,512]{2,1,0:T(2,128)S(1)} %neg.37, f32[8,2,512]{2,1,0:T(2,128)S(1)} %fusion.73, pred[512,512]{0,1:T(8,128)(4,1)S(1)} %iota_compare_fusion, ...), kind=kOutput, calls=%fused_computation.106 | convolution fusion | flops 1112014848 | bytes 28672000 | tf_op jit(solution)/shard_map/transpose(jvp(bqkgd,bskd->bkgqs))/dot_general | solution.py:44
  293.8 9.4 convert_bitcast_fusion.2
  310.7 6.2 copy.342
  353.6 6.0 multiply_reduce_fusion.3
  391.8 7.0 copy.352
  398.7 6.4 multiply_add_fusion.1
  410.5 8.1 copy.356
  423.2 7.5 reshape.385
  430.7 17.0 %multiply_reduce_fusion = (f32[16,64,2]{2,1,0:T(8,128)}, f32[8,64,16]{1,0,2:T(8,128)S(1)}) fusion(f32[8,64,16,64,2]{1,0,4,3,2:T(8,128)} %reshape.391, f32[8,64,16]{1,0,2:T(8,128)S(1)} %copy-done.51, f32[8,64,16]{1,0,2:T(8,128)S(1)} %copy-done.49, f32[8,64,16,64,1]{1,0,4,3,2:T(8,128)} %get-tuple-element.103, f32[8,64,16,64,1]{1,0,4,3,2:T(8,128)} %copy-done.8, ...), kind=kLoop, calls=%fused_computation.22 | loop fusion | flops 11524096 | bytes 8536064 | tf_op jit(solution)/shard_map/transpose(jvp())/reduce_sum | solution.py:28
  459.0 10.6 fusion.25
  469.6 7.7 fusion.92
  491.4 6.3 convolution_convert_fusion.7
  503.5 9.4 add_convert_fusion.2
  516.5 627.3 %all-reduce.6 = (bf16[1024,2048]{1,0:T(8,128)(2,1)}, bf16[1024,1024]{1,0:T(8,128)(2,1)}, bf16[1024,1024]{1,0:T(8,128)(2,1)}, bf16[2048,1024]{1,0:T(8,128)(2,1)},...) all-reduce(f32[1024,2048]{1,0:T(8,128)} %fusion.92, ...), channel_id=1, replica_groups=mesh['dp'=4,'sp'=8] {'sp'}, use_global_device_ids=true, to_apply=%region_15.16 | all-reduce | flops 15732736 | bytes 94404608 | tf_op jit(solution)/shard_map/psum | solution.py:125
  (315 shorter events, 252.1 us)
Async XLA Ops:
  0.6 118.2 %copy-start = (bf16[1024,1024]{1,0:T(8,128)(2,1)S(1)}, bf16[1024,1024]{1,0:T(8,128)(2,1)}, u32[]{:S(2)}) copy-start(bf16[1024,1024]{1,0:T(8,128)(2,1)} %param.18) | copy-start | bytes 6291460
  6.2 161.0 %copy-start.19 = (bf16[8,64,1024]{2,1,0:T(8,128)(2,1)}, bf16[8,64,1024]{2,1,0:T(8,128)(2,1)S(1)}, u32[]{:S(2)}) copy-start(bf16[8,64,1024]{2,1,0:T(8,128)(2,1)S(1)} %fusion.34) | copy-start | bytes 3145732
  16.6 15.1 %copy-start.24 = (f32[8,64,2]{2,1,0:T(8,128)}, f32[8,64,2]{2,1,0:T(8,128)S(1)}, u32[]{:S(2)}) copy-start(f32[8,64,2]{2,1,0:T(8,128)S(1)} %copy.325) | copy-start | bytes 12292
  28.0 112.2 %copy-start.46 = (f32[8,64,8]{1,2,0:T(8,128)}, f32[8,64,8]{1,2,0:T(8,128)S(1)}, u32[]{:S(2)}) copy-start(f32[8,64,8]{1,2,0:T(8,128)S(1)} %broadcast_multiply_fusion.1) | copy-start | bytes 49156
  31.8 100.0 %copy-start.42 = (f32[64,64]{0,1:T(8,128)}, f32[64,64]{0,1:T(8,128)S(1)}, u32[]{:S(2)}) copy-start(f32[64,64]{0,1:T(8,128)S(1)} %get-tuple-element.112) | copy-start | bytes 49156
  31.8 100.0 %copy-start.44 = (f32[64,64]{0,1:T(8,128)}, f32[64,64]{0,1:T(8,128)S(1)}, u32[]{:S(2)}) copy-start(f32[64,64]{0,1:T(8,128)S(1)} %get-tuple-element.113) | copy-start | bytes 49156
  38.4 87.8 %all-to-all-start.1 = ((bf16[8,64,8,128]{3,1,0,2:T(8,128)(2,1)}), bf16[8,64,8,128]{3,1,0,2:T(8,128)(2,1)}, u32[]{:S(2)}, u32[]{:S(2)}) async-start(bf16[8,64,8,128]{3,1,0,2:T(8,128)(2,1)} %copy.327), calls=%async_computation.1 | async-start | bytes 2097152 | tf_op jit(solution)/shard_map/all_to_all | solution.py:84
  100.7 37.7 %copy-start.29 = (f32[8,64,16]{1,2,0:T(8,128)}, f32[8,64,16]{1,2,0:T(8,128)S(1)}, u32[]{:S(2)}) copy-start(f32[8,64,16]{1,2,0:T(8,128)S(1)} %broadcast_multiply_fusion) | copy-start | bytes 98308
  100.7 20.9 %copy-start.48 = (f32[8,64,16]{1,0,2:T(8,128)}, f32[8,64,16]{1,0,2:T(8,128)S(1)}, u32[]{:S(2)}) copy-start(f32[8,64,16]{1,0,2:T(8,128)S(1)} %copy.331) | copy-start | bytes 98308
  106.0 15.6 %slice-start = ((s8[8388608]{0:T(1024)(128)(4,1)}), s8[4194304]{0:T(1024)(128)(4,1)S(1)}, s32[]{:S(2)}) async-start(s8[8388608]{0:T(1024)(128)(4,1)} %bitcast.300), calls=%async_computation.8 | async-start | bytes 8388608
  106.1 15.6 %copy-start.50 = (f32[8,64,16]{1,0,2:T(8,128)}, f32[8,64,16]{1,0,2:T(8,128)S(1)}, u32[]{:S(2)}) copy-start(f32[8,64,16]{1,0,2:T(8,128)S(1)} %copy.333) | copy-start | bytes 98308
  106.1 15.6 %slice-start.1 = ((s8[8388608]{0:T(1024)(128)(4,1)}), s8[4194304]{0:T(1024)(128)(4,1)S(1)}, s32[]{:S(2)}) async-start(s8[8388608]{0:T(1024)(128)(4,1)} %bitcast.300), calls=%async_computation.9 | async-start | bytes 8388608
  126.3 36.1 %all-to-all-start = ((bf16[8,64,8,128]{3,1,0,2:T(8,128)(2,1)}), bf16[8,64,8,128]{3,1,0,2:T(8,128)(2,1)}, u32[]{:S(2)}, u32[]{:S(2)}) async-start(bf16[8,64,8,128]{3,1,0,2:T(8,128)(2,1)} %copy.317), calls=%async_computation | async-start | bytes 2097152 | tf_op jit(solution)/shard_map/all_to_all | solution.py:85
  162.4 30.9 %all-to-all-start.4 = ((bf16[8,64,16,128]{3,1,0,2:T(8,128)(2,1)}), bf16[8,64,16,128]{3,1,0,2:T(8,128)(2,1)}, u32[]{:S(2)}, u32[]{:S(2)}) async-start(bf16[8,64,16,128]{3,1,0,2:T(8,128)(2,1)} %copy.345), calls=%async_computation.4 | async-start | bytes 4194304 | tf_op jit(solution)/shard_map/all_to_all | solution.py:105
  167.2 11.0 copy-start.32
  167.2 11.0 copy-start.81
  193.3 32.2 %all-to-all-start.2 = ((bf16[8,64,16,128]{3,1,0,2:T(8,128)(2,1)}), bf16[8,64,16,128]{3,1,0,2:T(8,128)(2,1)}, u32[]{:S(2)}, u32[]{:S(2)}) async-start(bf16[8,64,16,128]{3,1,0,2:T(8,128)(2,1)} %copy.337), calls=%async_computation.2 | async-start | bytes 4194304 | tf_op jit(solution)/shard_map/all_to_all | solution.py:83
  199.0 8.7 copy-start.82
  243.9 9.9 copy-start.27
  243.9 9.9 copy-start.40
  262.8 12.6 %copy-start.15 = (bf16[8,8,64,2,128]{4,2,1,3,0:T(8,128)(2,1)S(1)}, bf16[8,8,64,2,128]{4,2,1,3,0:T(8,128)(2,1)}, u32[]{:S(2)}) copy-start(bf16[8,8,64,2,128]{4,2,1,3,0:T(8,128)(2,1)} %copy-done.14) | copy-start | bytes 6291460
  288.9 27.9 %all-to-all-start.6 = ((bf16[8,512,1,128]{3,0,2,1:T(8,128)(2,1)}), bf16[8,512,1,128]{3,0,2,1:T(8,128)(2,1)S(1)}, u32[]{:S(2)}, u32[]{:S(2)}) async-start(bf16[8,512,1,128]{3,0,2,1:T(8,128)(2,1)} %copy.362), calls=%async_computation.6 | async-start | bytes 2097152 | tf_op jit(solution)/shard_map/all_to_all | solution.py:108
  317.8 27.9 %all-to-all-start.7 = ((bf16[8,512,1,128]{3,0,2,1:T(8,128)(2,1)}), bf16[8,512,1,128]{3,0,2,1:T(8,128)(2,1)S(1)}, u32[]{:S(2)}, u32[]{:S(2)}) async-start(bf16[8,512,1,128]{3,0,2,1:T(8,128)(2,1)} %copy.377), calls=%async_computation.7 | async-start | bytes 2097152 | tf_op jit(solution)/shard_map/all_to_all | solution.py:109
  345.7 36.0 %all-to-all-start.5 = ((bf16[8,512,2,128]{3,2,0,1:T(2,128)(2,1)}), bf16[8,512,2,128]{3,2,0,1:T(2,128)(2,1)}, u32[]{:S(2)}, u32[]{:S(2)}) async-start(bf16[8,512,2,128]{3,2,0,1:T(2,128)(2,1)} %copy.350), calls=%async_computation.5 | async-start | bytes 4194304 | tf_op jit(solution)/shard_map/all_to_all | solution.py:107
  381.8 99.3 %all-to-all-start.3 = ((bf16[8,512,2,128]{3,2,0,1:T(2,128)(2,1)}), bf16[8,512,2,128]{3,2,0,1:T(2,128)(2,1)}, u32[]{:S(2)}, u32[]{:S(2)}) async-start(bf16[8,512,2,128]{3,2,0,1:T(2,128)(2,1)} %copy.342), calls=%async_computation.3 | async-start | bytes 4194304 | tf_op jit(solution)/shard_map/all_to_all | solution.py:90
  407.2 11.4 slice-start.2
  410.4 8.2 copy-start.1
  503.4 9.5 copy-start.3
  503.4 9.5 copy-start.65
  503.5 9.5 copy-start.66
  503.5 10.0 copy-start.70
  503.5 10.4 copy-start.68
  (68 other events, 305.1 us)
where the time goes:
time: 1160 us; the launch traced here: 1150 us
  blocking collectives  627 us (54%)
  matrix products  188 us (16%)
  local copies, waits for them, and re-layouts  169 us (15%)
  other arithmetic  111 us (10%)
  starting transfers between devices  43.2 us (4%)
    psum x1, blocking collectives, layer_step(): lax.psum(part_grad, 'sp').astype(jnp.bfloat16)  627 us
    dot_general x7, matrix products, grad_product(): lax.dot_general(act_rows, grad_rows, (((0,), (0,)), ((), ())), preferred_...  45.9 us
    dot_general x7, matrix products, times_transposed(): lax.dot_general(lhs_mat, rhs_mat, (((1,), (1,)), ((), ())), preferred_ele...  39.8 us
    dot_general x3, matrix products, attend(): jnp.einsum('bqkgd,bskd->bkgqs', q_rot, k_rot, preferred_element_type=jnp....  31.7 us
    convert_element_type x6, local copies, waits for them, and re-layouts, head_prepare(): proj_f32 = proj_in.astype(jnp.float32)  31.3 us
    dot_general x3, matrix products, attend(): jnp.einsum('bkgqs,bskd->bqkgd', attn_probs, v_proj, preferred_element_typ...  28.3 us
    reduce_sum x4, other arithmetic, head_prepare(): normed = centered * lax.rsqrt(row_var + NORM_EPS) * norm_weight  28 us
    unnamed x194, local copies, waits for them, and re-layouts  25 us
  transfers between devices with their start and end apart: 8, of which 1 were waited for; matrix products, arithmetic and copies ran while one was open for 28% of the time, Pallas kernels for 0%

commit v1 on v0

v1 whole, which is shorter than its diff:
```python
import functools

import jax
import jax.numpy as jnp
from jax import lax
from jax.experimental import pallas as pl
from jax.experimental.pallas import tpu as pltpu
from jax.sharding import PartitionSpec as P

NORM_EPS = 1e-5
ROPE_THETA = 75.0e6
F32 = jnp.float32
BF16 = jnp.bfloat16


def dot_nn(lhs, rhs):
    return lax.dot_general(lhs, rhs, (((1,), (0,)), ((), ())), preferred_element_type=F32)


def dot_nt(lhs, rhs):
    return lax.dot_general(lhs, rhs, (((1,), (1,)), ((), ())), preferred_element_type=F32)


def dot_tn(lhs, rhs):
    return lax.dot_general(lhs, rhs, (((0,), (0,)), ((), ())), preferred_element_type=F32)


def input_norm(x_f32, norm_gain):
    row_mean = jnp.mean(x_f32, axis=-1, keepdims=True)
    centered = x_f32 - row_mean
    row_var = jnp.mean(centered * centered, axis=-1, keepdims=True)
    return (centered * lax.rsqrt(row_var + NORM_EPS) * norm_gain).astype(BF16)


def swiglu(gate_pre, up_proj):
    return (jax.nn.silu(gate_pre) * up_proj).astype(BF16)


def swap_pairs(rows):
    width = rows.shape[1]
    lane = lax.broadcasted_iota(jnp.int32, rows.shape, 1)
    return jnp.where(lane % 2 == 0, pltpu.roll(rows, width - 1, 1), pltpu.roll(rows, 1, 1))


def head_forward(rows, weight, cos_t, sin_t):
    rows = rows.astype(F32)
    centered = rows - jnp.mean(rows, axis=-1, keepdims=True)
    scale = lax.rsqrt(jnp.mean(centered * centered, axis=-1, keepdims=True) + NORM_EPS)
    unit = centered * scale
    normed = unit * weight
    return (normed * cos_t + swap_pairs(normed) * sin_t).astype(BF16), unit, scale


def head_backward(grad, unit, scale, weight, cos_t, sin_t):
    grad = grad.astype(BF16).astype(F32)
    grad = grad * cos_t - swap_pairs(grad) * sin_t
    weight_grad = jnp.sum(grad * unit, axis=0, keepdims=True)
    grad = grad * weight
    along = jnp.mean(grad * unit, axis=-1, keepdims=True)
    grad = scale * (grad - jnp.mean(grad, axis=-1, keepdims=True) - unit * along)
    return grad.astype(BF16), weight_grad


def attention_kernel(qkv_ref, do_ref, cos_ref, sin_ref, qn_ref, kn_ref, o_ref, dqkv_ref, wn_ref, k_acc, v_acc, *, heads, dim, block):
    pieces, _, piece, _ = qkv_ref.shape
    full = pieces * piece
    cos_t, sin_t = cos_ref[...], sin_ref[...]
    score_scale = dim ** -0.5
    width = heads * dim

    def columns(ref, start, size):
        return ref[:, 0, :, start:start + size].reshape(full, size)

    def put(ref, start, rows):
        ref[:, 0, :, start:start + rows.shape[1]] = rows.reshape(pieces, piece, rows.shape[1])

    q_parts = [head_forward(columns(qkv_ref, h * dim, dim), qn_ref[h:h + 1, :], cos_t, sin_t) for h in range(heads)]
    k_rot, k_unit, k_scale = head_forward(columns(qkv_ref, width, dim), kn_ref[...], cos_t, sin_t)
    v_rows = columns(qkv_ref, width + dim, dim)
    do_parts = [columns(do_ref, h * dim, dim) for h in range(heads)]
    k_acc[...] = jnp.zeros_like(k_acc)
    v_acc[...] = jnp.zeros_like(v_acc)
    o_blocks, dq_blocks = [[] for _ in range(heads)], [[] for _ in range(heads)]
    for start in range(0, full, block):
        stop = start + block
        q_blk = jnp.concatenate([q_parts[h][0][start:stop] for h in range(heads)], axis=0)
        do_blk = jnp.concatenate([do_parts[h][start:stop] for h in range(heads)], axis=0)
        k_blk, v_blk = k_rot[:stop], v_rows[:stop]
        scores = dot_nt(q_blk, k_blk) * score_scale
        row = lax.broadcasted_iota(jnp.int32, scores.shape, 0) % block + start
        scores = jnp.where(row >= lax.broadcasted_iota(jnp.int32, scores.shape, 1), scores, -1e30)
        probs = jnp.exp(scores - jnp.max(scores, axis=-1, keepdims=True))
        probs = probs / jnp.sum(probs, axis=-1, keepdims=True)
        probs_b = probs.astype(BF16)
        o_blk = dot_nn(probs_b, v_blk).astype(BF16)
        d_probs = dot_nt(do_blk, v_blk)
        delta = jnp.sum(probs * d_probs, axis=-1, keepdims=True)
        d_scores = (probs * (d_probs - delta) * score_scale).astype(BF16)
        dq_blk = dot_nn(d_scores, k_blk)
        k_acc[0:stop, :] += dot_tn(d_scores, q_blk)
        v_acc[0:stop, :] += dot_tn(probs_b, do_blk)
        for h in range(heads):
            o_blocks[h].append(o_blk[h * block:(h + 1) * block])
            dq_blocks[h].append(dq_blk[h * block:(h + 1) * block])
    weight_grads = []
    for h in range(heads):
        put(o_ref, h * dim, jnp.concatenate(o_blocks[h], axis=0))
        _, unit, scale = q_parts[h]
        dq, weight_grad = head_backward(jnp.concatenate(dq_blocks[h], axis=0), unit, scale, qn_ref[h:h + 1, :], cos_t, sin_t)
        put(dqkv_ref, h * dim, dq)
        weight_grads.append(weight_grad)
    dk, weight_grad = head_backward(k_acc[...], k_unit, k_scale, kn_ref[...], cos_t, sin_t)
    put(dqkv_ref, width, dk)
    put(dqkv_ref, width + dim, v_acc[...].astype(BF16))
    weight_grads.append(weight_grad)

    @pl.when(pl.program_id(0) == 0)
    def _():
        wn_ref[...] = jnp.zeros_like(wn_ref)

    for i, weight_grad in enumerate(weight_grads):
        wn_ref[i:i + 1, :] += weight_grad


def attention(qkv, d_out, cos_t, sin_t, q_norm, k_norm):
    pieces, batch, piece, _ = qkv.shape
    heads, dim = q_norm.shape
    full = pieces * piece
    block = min(128, full)
    seq = lambda width: pl.BlockSpec((pieces, 1, piece, width), lambda b: (0, b, 0, 0))
    whole = lambda shape: pl.BlockSpec(shape, lambda b: (0,) * len(shape))
    return pl.pallas_call(
        functools.partial(attention_kernel, heads=heads, dim=dim, block=block),
        grid=(batch,),
        in_specs=[seq((heads + 2) * dim), seq(heads * dim), whole((full, dim)), whole((full, dim)), whole((heads, dim)), whole((1, dim))],
        out_specs=[seq(heads * dim), seq((heads + 2) * dim), whole((8, dim))],
        out_shape=[jax.ShapeDtypeStruct((pieces, batch, piece, heads * dim), BF16),
                   jax.ShapeDtypeStruct((pieces, batch, piece, (heads + 2) * dim), BF16),
                   jax.ShapeDtypeStruct((8, dim), F32)],
        scratch_shapes=[pltpu.VMEM((full, dim), F32), pltpu.VMEM((full, dim), F32)],
        cost_estimate=pl.CostEstimate(flops=14 * batch * heads * full * full * dim, bytes_accessed=batch * full * dim * 26, transcendentals=0),
    )(qkv, d_out, cos_t, sin_t, q_norm, k_norm)


def solution(mesh):
    n_sp = mesh.shape['sp']
    seq_spec = P('dp', 'sp', None)
    grad_spec = P('dp', None)

    def layer_step(x_in, grad_y, positions, w_q, w_k, w_v, w_o, w_gate, w_up, w_down, norm_gain, q_norm, k_norm):
        batch, piece, model = x_in.shape
        num_heads, dim = q_norm.shape
        num_kv = k_norm.shape[0]
        heads = num_heads // num_kv
        ffn = w_gate.shape[1]
        tokens = batch * piece
        me = lax.axis_index('sp')
        x_f32 = x_in.astype(F32)
        normed, norm_back = jax.vjp(input_norm, x_f32, norm_gain)
        dy_all = lax.all_gather(grad_y, 'sp', axis=0, tiled=False)
        n_all = lax.all_gather(normed, 'sp', axis=0, tiled=False)
        pos_all = lax.all_gather(positions, 'sp', axis=0, tiled=True)
        flat_norm = normed.reshape(tokens, model)
        flat_grad = grad_y.reshape(tokens, model)
        n_rows = n_all.reshape(n_sp * tokens, model)
        dy_rows = dy_all.reshape(n_sp * tokens, model)

        inv_freq = ROPE_THETA ** (-(jnp.arange(dim // 2, dtype=F32) * 2.0) / dim)
        angles = jnp.repeat(pos_all.astype(F32)[:, None] * inv_freq[None, :], 2, axis=1)
        sign = jnp.where(jnp.arange(dim) % 2 == 0, -1.0, 1.0).astype(F32)
        cos_t, sin_t = jnp.cos(angles), jnp.sin(angles) * sign[None, :]

        gate_pre = dot_nn(flat_norm, w_gate)
        up_proj = dot_nn(flat_norm, w_up)
        hidden, act_back = jax.vjp(swiglu, gate_pre, up_proj)
        mlp_out = dot_nn(hidden, w_down).astype(BF16)
        d_gate, d_up = act_back(dot_nt(flat_grad, w_down).astype(BF16))
        d_norm = dot_nt(d_gate.astype(BF16), w_gate) + dot_nt(d_up.astype(BF16), w_up)

        wq_mine = lax.dynamic_slice_in_dim(w_q, me * heads * dim, heads * dim, 1)
        wk_mine = lax.dynamic_slice_in_dim(w_k, me * dim, dim, 1)
        wv_mine = lax.dynamic_slice_in_dim(w_v, me * dim, dim, 1)
        wo_mine = lax.dynamic_slice_in_dim(w_o, me * heads * dim, heads * dim, 0)
        qkv = dot_nn(n_rows, jnp.concatenate([wq_mine, wk_mine, wv_mine], axis=1)).astype(BF16)
        d_attn = dot_nt(dy_rows, wo_mine).astype(BF16)
        qn_mine = lax.dynamic_slice_in_dim(q_norm, me * heads, heads, 0)
        kn_mine = lax.dynamic_slice_in_dim(k_norm, me, 1, 0)
        o_heads, dqkv, norm_grads = attention(qkv.reshape(n_sp, batch, piece, -1), d_attn.reshape(n_sp, batch, piece, -1), cos_t, sin_t, qn_mine, kn_mine)
        o_seq = lax.all_to_all(o_heads, 'sp', 0, 0, tiled=True)
        dqkv_seq = lax.all_to_all(dqkv, 'sp', 0, 0, tiled=True)
        dqkv_rows = dqkv.reshape(n_sp * tokens, -1)
        o_rows = o_heads.reshape(n_sp * tokens, -1)
        grad_qkv = dot_tn(n_rows, dqkv_rows).astype(BF16)
        grad_o = dot_tn(o_rows, dy_rows).astype(BF16)

        share = ffn // n_sp
        wg_mine = lax.dynamic_slice_in_dim(w_gate, me * share, share, 1)
        wu_mine = lax.dynamic_slice_in_dim(w_up, me * share, share, 1)
        wd_mine = lax.dynamic_slice_in_dim(w_down, me * share, share, 0)
        hid_cols, cols_back = jax.vjp(swiglu, dot_nn(n_rows, wg_mine), dot_nn(n_rows, wu_mine))
        dg_cols, du_cols = cols_back(dot_nt(dy_rows, wd_mine).astype(BF16))
        grad_gate = dot_tn(n_rows, dg_cols.astype(BF16)).astype(BF16)
        grad_up = dot_tn(n_rows, du_cols.astype(BF16)).astype(BF16)
        grad_down = dot_tn(hid_cols, dy_rows).astype(BF16)
        full_gate = lax.all_gather(grad_gate, 'sp', axis=1, tiled=True)
        full_up = lax.all_gather(grad_up, 'sp', axis=1, tiled=True)
        full_down = lax.all_gather(grad_down, 'sp', axis=0, tiled=True)
        full_o = lax.all_gather(grad_o, 'sp', axis=0, tiled=True)
        full_qkv = lax.all_gather(grad_qkv, 'sp', axis=0, tiled=False)
        unstack = lambda part: jnp.moveaxis(part, 0, 1).reshape(model, -1)
        full_q = unstack(full_qkv[:, :, :heads * dim])
        full_k = unstack(full_qkv[:, :, heads * dim:(heads + 1) * dim])
        full_v = unstack(full_qkv[:, :, (heads + 1) * dim:])

        o_seq = o_seq.reshape(n_sp, tokens, heads * dim)
        attn_out = lax.dot_general(o_seq, w_o.reshape(n_sp, heads * dim, model), (((0, 2), (0, 1)), ((), ())), preferred_element_type=F32).astype(BF16)
        y_out = (x_f32 + attn_out.astype(F32).reshape(x_in.shape) + mlp_out.astype(F32).reshape(x_in.shape)).astype(BF16)
        dqkv_seq = dqkv_seq.reshape(n_sp, tokens, -1)

        def back_rows(start, size, weight):
            return lax.dot_general(dqkv_seq[:, :, start:start + size], weight.reshape(model, n_sp, size), (((0, 2), (1, 2)), ((), ())), preferred_element_type=F32)

        d_norm = d_norm + back_rows(0, heads * dim, w_q) + back_rows(heads * dim, dim, w_k) + back_rows((heads + 1) * dim, dim, w_v)
        dx_norm, grad_gain = norm_back(d_norm.astype(BF16).reshape(x_in.shape))
        grad_x = (grad_y.astype(F32) + dx_norm).astype(BF16)

        small = jnp.concatenate([grad_gain.reshape(-1, dim), norm_grads[:heads + 1]], axis=0)
        small = lax.all_gather(small, 'sp', axis=0, tiled=False)
        gain_rows = model // dim
        full_gain = jnp.sum(small[:, :gain_rows], axis=0).reshape(model)
        full_qn = small[:, gain_rows:gain_rows + heads].reshape(num_heads, dim)
        full_kn = small[:, gain_rows + heads]
        return y_out, grad_x, full_q, full_k, full_v, full_o, full_gate, full_up, full_down, full_gain, full_qn, full_kn

    in_specs = (seq_spec, seq_spec, P(('dp', 'sp'))) + (P(),) * 10
    out_specs = (seq_spec, seq_spec) + (grad_spec,) * 7 + (P('dp'), grad_spec, grad_spec)
    return jax.shard_map(layer_step, mesh=mesh, in_specs=in_specs, out_specs=out_specs, check_vma=False)
```

time: 1160 us -> 477 us (0.41)
  blocking collectives: 627 us -> 22.9 us
  waiting for transfers between devices: 8.61 us -> 151 us
  local copies, waits for them, and re-layouts: 169 us -> 41 us
  other arithmetic: 111 us -> 11.5 us
  Pallas kernels: 0 us -> 61.2 us
  starting transfers between devices: 43.2 us -> 10.6 us
  matrix products: 188 us -> 158 us
  between operations: 2.44 us -> 15.7 us
    psum x1 -> x0, blocking collectives: 627 us -> none  [layer_step(): lax.psum(part_grad, 'sp').astype(jnp.bfloat16)]
    all_gather x0 -> x7, waiting for transfers between devices: none -> 76.2 us  [the longest x1 40.3 us: layer_step(): n_all = lax.all_gather(normed, 'sp', axis=0, tiled=False)]
    all_to_all x8 -> x2, waiting for transfers between devices: 8.61 us -> 73.7 us  [the longest x1 47.4 us: layer_step(): dqkv_seq = lax.all_to_all(dqkv, 'sp', 0, 0, tiled=True)]
    pallas_call x0 -> x1, Pallas kernels: none -> 61.2 us  [attention(): pl.pallas_call(functools.partial(attention_kernel, heads=heads, dim=dim,...]
    convert_element_type x13 -> x1, local copies, waits for them, and re-layouts: 59.3 us -> 2.67 us  [layer_step(): d_attn = dot_nt(dy_rows, wo_mine).astype(BF16)]
    reduce_sum x11 -> x3, other arithmetic: 52.6 us -> 2.23 us  [the longest x2 1.63 us: input_norm(): return (centered * lax.rsqrt(row_var + NORM_EPS) * norm_gain).astype(BF16)]
    all_to_all x8 -> x2, starting transfers between devices: 43.2 us -> 9.3 us  [the longest x1 5.4 us: layer_step(): dqkv_seq = lax.all_to_all(dqkv, 'sp', 0, 0, tiled=True)]
    reshape x8 -> x3, local copies, waits for them, and re-layouts: 37.2 us -> 6.44 us  [layer_step(): unstack = lambda part: jnp.moveaxis(part, 0, 1).reshape(model, -1)]
  transfers between devices with their start and end apart: 8 -> 9, of which waited for: 1 -> 5; matrix products, arithmetic and copies ran while one was open for 28% -> 34% of each run, Pallas kernels for 0% -> 0%
where the time goes in v1:
time: 477 us; the launch traced here: 472 us
  matrix products  158 us (33%)
  waiting for transfers between devices  151 us (32%)
  Pallas kernels  61.2 us (13%)
  local copies, waits for them, and re-layouts  41 us (9%)
  blocking collectives  22.9 us (5%)
  between operations  15.7 us (3%)
  other arithmetic  11.5 us (2%)
  starting transfers between devices  10.6 us (2%)
    pallas_call x1, Pallas kernels, attention(): pl.pallas_call(functools.partial(attention_kernel, heads=heads, dim=dim,...  61.2 us
    dot_general x6, matrix products, dot_nn(): lax.dot_general(lhs, rhs, (((1,), (0,)), ((), ())), preferred_element_typ...  50.6 us
    dot_general x5, matrix products, dot_tn(): lax.dot_general(lhs, rhs, (((0,), (0,)), ((), ())), preferred_element_typ...  48 us
    all_to_all x1, waiting for transfers between devices, layer_step(): dqkv_seq = lax.all_to_all(dqkv, 'sp', 0, 0, tiled=True)  47.4 us
    dot_general x5, matrix products, dot_nt(): lax.dot_general(lhs, rhs, (((1,), (1,)), ((), ())), preferred_element_typ...  45.4 us
    all_gather x1, waiting for transfers between devices, layer_step(): n_all = lax.all_gather(normed, 'sp', axis=0, tiled=False)  40.3 us
    all_gather x1, waiting for transfers between devices, layer_step(): dy_all = lax.all_gather(grad_y, 'sp', axis=0, tiled=False)  28.4 us
    all_to_all x1, waiting for transfers between devices, layer_step(): o_seq = lax.all_to_all(o_heads, 'sp', 0, 0, tiled=True)  26.3 us
  transfers between devices with their start and end apart: 9, of which 5 were waited for; matrix products, arithmetic and copies ran while one was open for 34% of the time, Pallas kernels for 0%

profile of v1, /device:TPU:81, one launch (start us, length us, event | category | flops | bytes accessed | tf_op | source)
XLA Modules:
  0.0 471.9 jit_solution(13598156801162721605)
XLA Ops:
  16.6 8.9 %all-reduce = s32[512]{0:T(512)S(1)} all-reduce(s32[512]{0:T(512)S(1)} %dynamic-update-slice), channel_id=1, replica_groups=mesh['dp'=4,'sp'=8] {'sp'}, use_global_device_ids=true, to_apply=%add | all-reduce | flops 512 | bytes 4096
  32.3 28.4 %all-gather.23.cloned.1.call-done = bf16[64,64,1024]{2,1,0:T(8,128)(2,1)} async-done(((bf16[8,64,1024]{2,1,0:T(8,128)(2,1)}), bf16[64,64,1024]{2,1,0:T(8,128)(2,1)}) %all-gather.23.cloned.1.call-update) | async-done | bytes 8388624 | tf_op jit(solution)/shard_map/all_gather | solution.py:160
  60.8 5.9 %fusion.10 = bf16[4096,256]{0,1:T(8,128)(2,1)S(1)} fusion(bf16[4096,1024]{1,0:T(8,128)(2,1)} %bitcast.131, bf16[2048,1024]{1,0:T(8,128)(2,1)} %param.19, s32[]{:T(128)S(6)} %select_n.38), kind=kOutput, calls=%fused_computation.23 | convolution fusion | flops 2148532224 | bytes 11010052 | tf_op jit(solution)/shard_map/dot_general | solution.py:21
  69.4 40.3 %all-gather.21.cloned.1.call-done = bf16[64,64,1024]{2,1,0:T(8,128)(2,1)} async-done(((bf16[8,64,1024]{2,1,0:T(8,128)(2,1)}), bf16[64,64,1024]{2,1,0:T(8,128)(2,1)}) %all-gather.21.cloned.1.call-update) | async-done | bytes 8388624 | tf_op jit(solution)/shard_map/all_gather | solution.py:161
  109.7 9.6 %convolution_convert_fusion = bf16[4096,512]{1,0:T(8,128)(2,1)} fusion(bf16[4096,1024]{1,0:T(8,128)(2,1)} %bitcast.158, bf16[1024,128]{1,0:T(8,128)(2,1)S(1)} %get-tuple-element.26, bf16[1024,128]{1,0:T(8,128)(2,1)S(1)} %get-tuple-element.27, bf16[1024,256]{1,0:T(8,128)(2,1)S(1)} %constant_dynamic-slice_fusion.4), kind=kOutput, calls=%fused_computation.20 | convolution fusion | flops 4300210176 | bytes 13631488 | tf_op jit(solution)/shard_map/dot_general | solution.py:17
  119.3 61.2 %shard_map.220 = (bf16[8,8,64,256]{3,2,1,0:T(8,128)(2,1)}, bf16[8,8,64,512]{3,2,1,0:T(8,128)(2,1)}, f32[8,128]{1,0:T(8,128)}) custom-call(bf16[8,8,64,512]{3,2,1,0:T(8,128)(2,1)} %bitcast.167, bf16[8,8,64,256]{3,2,1,0:T(8,128)(2,1)} %bitcast.150, f32[512,128]{1,0:T(8,128)} %copy.54.cos_ref, f32[512,128]{1,0:T(8,128)} %broadcast_multiply_fusion.sin_ref, ...), custom_call_target="tpu_custom_call" | custom-call | flops 7516192768 | bytes 13631488 | tf_op jit(solution)/shard_map/pallas_call | solution.py:132
  180.5 7.2 %fusion.55 = bf16[256,1024]{1,0:T(8,128)(2,1)} fusion(bf16[8,8,64,256]{3,2,1,0:T(8,128)(2,1)} %get-tuple-element.15, bf16[8,8,64,1024]{3,2,1,0:T(8,128)(2,1)} %bitcast.132), kind=kOutput, calls=%fused_computation.77 | convolution fusion | flops 2147745792 | bytes 11010048 | tf_op jit(solution)/shard_map/dot_general | solution.py:25
  188.1 8.8 %convolution_convert_fusion.1 = bf16[384,4096]{1,0:T(8,128)(2,1)} fusion(bf16[4096,1024]{1,0:T(8,128)(2,1)} %bitcast.133, bf16[3072,1024]{1,0:T(8,128)(2,1)} %param.22, s32[]{:T(128)S(6)} %select_n.44), kind=kOutput, calls=%fused_computation.21 | convolution fusion | flops 3222798336 | bytes 12320772 | tf_op jit(solution)/shard_map/dot_general | solution.py:21
  196.9 6.9 %fusion.67 = f32[4096,384]{0,1:T(8,128)S(1)} fusion(bf16[4096,1024]{1,0:T(8,128)(2,1)} %bitcast.159, bf16[1024,3072]{1,0:T(8,128)(2,1)} %param.20, s32[]{:T(128)S(6)} %select_n.44), kind=kOutput, calls=%fused_computation.85 | convolution fusion | flops 3221225472 | bytes 15466500 | tf_op jit(solution)/shard_map/dot_general | solution.py:17
  203.8 8.5 %fusion.69 = f32[4096,384]{0,1:T(8,128)S(1)} fusion(bf16[4096,1024]{1,0:T(8,128)(2,1)} %bitcast.160, bf16[1024,3072]{1,0:T(8,128)(2,1)} %param.21, s32[]{:T(128)S(6)} %select_n.44), kind=kOutput, calls=%fused_computation.87 | convolution fusion | flops 3221225472 | bytes 15466500 | tf_op jit(solution)/shard_map/dot_general | solution.py:17
  215.0 7.6 %fusion.48 = bf16[1024,384]{1,0:T(8,128)(2,1)} fusion(bf16[4096,1024]{1,0:T(8,128)(2,1)S(1)} %bitcast.165, f32[4096,384]{0,1:T(8,128)S(1)} %fusion.67, f32[4096,384]{0,1:T(8,128)S(1)} %fusion.69, bf16[384,4096]{1,0:T(8,128)(2,1)} %convolution_convert_fusion.1), kind=kOutput, calls=%fused_computation.73 | convolution fusion | flops 3240493056 | bytes 24903680 | tf_op jit(solution)/shard_map/dot_general | solution.py:25
  223.2 11.6 %fusion.51 = bf16[1024,384]{1,0:T(8,128)(2,1)} fusion(bf16[4096,1024]{1,0:T(8,128)(2,1)} %bitcast.161, bf16[384,4096]{1,0:T(8,128)(2,1)} %convolution_convert_fusion.1, f32[4096,384]{0,1:T(8,128)} %copy-done.25), kind=kOutput, calls=%fused_computation.74 | convolution fusion | flops 3232628736 | bytes 18612224 | tf_op jit(solution)/shard_map/dot_general | solution.py:25
  235.0 11.4 %fusion.47 = bf16[384,1024]{1,0:T(8,128)(2,1)} fusion(bf16[4096,1024]{1,0:T(8,128)(2,1)} %bitcast.134, f32[4096,384]{0,1:T(8,128)} %copy-done.26, f32[4096,384]{0,1:T(8,128)} %copy-done.25), kind=kOutput, calls=%fused_computation.72 | convolution fusion | flops 3231055872 | bytes 21757952 | tf_op jit(solution)/shard_map/dot_general | solution.py:25
  246.7 10.1 %bitcast_convert_fusion = bf16[1024,512]{1,0:T(8,128)(2,1)} fusion(bf16[8,8,64,1024]{3,2,1,0:T(8,128)(2,1)} %bitcast.162, bf16[8,8,64,512]{3,2,1,0:T(8,128)(2,1)} %get-tuple-element.16), kind=kOutput, calls=%fused_computation.64 | convolution fusion | flops 4295491584 | bytes 13631488 | tf_op jit(solution)/shard_map/dot_general | solution.py:25
  256.9 8.1 %fusion.85 = f32[512,3072]{1,0:T(8,128)} fusion(bf16[512,1024]{1,0:T(8,128)(2,1)S(1)} %bitcast.145, bf16[1024,3072]{1,0:T(8,128)(2,1)} %param.20), kind=kOutput, calls=%fused_computation.120 | convolution fusion | flops 3221225472 | bytes 13631488 | tf_op jit(solution)/shard_map/dot_general | solution.py:17
  265.1 8.1 %fusion.86 = f32[512,3072]{1,0:T(8,128)} fusion(bf16[512,1024]{1,0:T(8,128)(2,1)S(1)} %bitcast.146, bf16[1024,3072]{1,0:T(8,128)(2,1)} %param.21), kind=kOutput, calls=%fused_computation.121 | convolution fusion | flops 3221225472 | bytes 13631488 | tf_op jit(solution)/shard_map/dot_general | solution.py:17
  273.2 3.9 all-to-all-start
  277.1 7.8 %convolution_convert_fusion.3 = bf16[512,3072]{1,0:T(8,128)(2,1)} fusion(bf16[512,1024]{1,0:T(8,128)(2,1)S(1)} %bitcast.143, bf16[3072,1024]{1,0:T(8,128)(2,1)} %param.22), kind=kOutput, calls=%fused_computation.24 | convolution fusion | flops 3222798336 | bytes 10485760 | tf_op jit(solution)/shard_map/dot_general | solution.py:21
  284.9 9.3 %fusion.46 = bf16[512,1024]{1,0:T(8,128)(2,1)} fusion(bf16[3072,1024]{1,0:T(8,128)(2,1)} %param.22, f32[512,3072]{1,0:T(8,128)S(1)} %copy-done.24, f32[512,3072]{1,0:T(8,128)} %fusion.85), kind=kOutput, calls=%fused_computation.71 | convolution fusion | flops 3231186944 | bytes 19922944 | tf_op jit(solution)/shard_map/dot_general | solution.py:17
  294.2 26.3 %all-to-all-done = bf16[8,8,64,256]{3,2,1,0:T(8,128)(2,1)S(1)} async-done(((bf16[8,8,64,256]{3,2,1,0:T(8,128)(2,1)}), bf16[8,8,64,256]{3,2,1,0:T(8,128)(2,1)S(1)}, u32[]{:S(2)}, u32[]{:S(2)}) %all-to-all-start) | async-done | bytes 2097184 | tf_op jit(solution)/shard_map/all_to_all | solution.py:189
  320.5 5.4 %all-to-all-start.1 = ((bf16[8,8,64,512]{3,2,1,0:T(8,128)(2,1)}), bf16[8,8,64,512]{3,2,1,0:T(8,128)(2,1)}, u32[]{:S(2)}, u32[]{:S(2)}) async-start(bf16[8,8,64,512]{3,2,1,0:T(8,128)(2,1)} %get-tuple-element.16), calls=%async_computation.1 | async-start | bytes 8388608 | tf_op jit(solution)/shard_map/all_to_all | solution.py:190
  325.9 10.5 %fusion.18 = f32[512,1024]{1,0:T(8,128)} fusion(bf16[1024,3072]{1,0:T(8,128)(2,1)} %param.21, bf16[512,3072]{1,0:T(8,128)(2,1)} %convolution_convert_fusion.3, f32[512,3072]{1,0:T(8,128)} %fusion.85), kind=kOutput, calls=%fused_computation.32 | convolution fusion | flops 3232235520 | bytes 17825792 | tf_op jit(solution)/shard_map/dot_general | solution.py:21
  336.4 12.5 %fusion.26 = f32[512,1024]{1,0:T(8,128)} fusion(bf16[1024,3072]{1,0:T(8,128)(2,1)} %param.20, f32[512,3072]{1,0:T(8,128)} %fusion.85, f32[512,3072]{1,0:T(8,128)} %fusion.86, bf16[512,3072]{1,0:T(8,128)(2,1)S(1)} %copy-done.27), kind=kOutput, calls=%fused_computation.42 | convolution fusion | flops 3240099840 | bytes 24117248 | tf_op jit(solution)/shard_map/dot_general | solution.py:21
  348.9 3.3 bitcast_convert_fusion.1
  352.2 47.4 %all-to-all-done.1 = bf16[8,8,64,512]{3,2,1,0:T(8,128)(2,1)} async-done(((bf16[8,8,64,512]{3,2,1,0:T(8,128)(2,1)}), bf16[8,8,64,512]{3,2,1,0:T(8,128)(2,1)}, u32[]{:S(2)}, u32[]{:S(2)}) %all-to-all-start.1) | async-done | bytes 4194336 | tf_op jit(solution)/shard_map/all_to_all | solution.py:190
  399.6 3.4 fusion.36
  403.1 4.2 fusion.11
  407.3 3.0 fusion.43
  412.1 13.9 %all-gather.4 = f32[8,11,128]{2,1,0:T(8,128)S(1)} all-gather(f32[1,11,128]{2,1,0:T(8,128)S(1)} %maximum_bitcast_fusion), channel_id=5, replica_groups=mesh['dp'=4,'sp'=8] {'sp'}, dimensions={0}, use_global_device_ids=true | all-gather | bytes 50688 | tf_op jit(solution)/shard_map/all_gather | solution.py:228
  430.2 7.5 %all-gather.25.cloned.1.call-done = bf16[8192,512]{1,0:T(8,128)(2,1)} async-done(((bf16[1024,512]{1,0:T(8,128)(2,1)}), bf16[8192,512]{1,0:T(8,128)(2,1)}) %all-gather.25.cloned.1.call-update) | async-done | bytes 8388624 | tf_op jit(solution)/shard_map/all_gather | solution.py:209
  453.6 3.2 copy.100
  457.5 3.2 copy.101
  (135 shorter events, 48.5 us)
Async XLA Ops:
  7.2 21.7 %copy-start = (f32[16,128]{1,0:T(8,128)S(1)}, f32[16,128]{1,0:T(8,128)}, u32[]{:S(2)}) copy-start(f32[16,128]{1,0:T(8,128)} %param.24) | copy-start | bytes 24580
  7.2 7.9 %copy-start.23 = (u32[32]{0:T(128)S(1)}, u32[32]{0:T(128)}, u32[]{:S(2)}) copy-start(u32[32]{0:T(128)} %constant.67) | copy-start | bytes 388
  7.2 9.1 %copy-start.22 = (s32[64]{0:T(128)S(1)}, s32[64]{0:T(128)}, u32[]{:S(2)}) copy-start(s32[64]{0:T(128)} %param.15) | copy-start | bytes 772
  7.2 53.5 %all-gather.23.cloned.1.call-start = ((), (), s32[]{:S(2)}) async-start(), calls=%async_computation.7 | async-start | bytes 9437184 | tf_op jit(solution)/shard_map/all_gather | solution.py:160
  8.0 101.6 %all-gather.21.cloned.1.call-start = ((), (), s32[]{:S(2)}) async-start(), calls=%async_computation.6 | async-start | bytes 9437184 | tf_op jit(solution)/shard_map/all_gather | solution.py:161
  15.0 415.2 %all-gather.13.cloned.1.call-start = ((), (), s32[]{:S(2)}) async-start(), calls=%async_computation.2 | async-start | bytes 4718592 | tf_op jit(solution)/shard_map/all_gather | solution.py:208
  187.8 242.4 %all-gather.15.cloned.1.call-start = ((), (), s32[]{:S(2)}) async-start(), calls=%async_computation.3 | async-start | bytes 7077888 | tf_op jit(solution)/shard_map/all_gather | solution.py:205
  196.9 18.2 %slice-start.6 = ((s8[8388608]{0:T(1024)(128)(4,1)}), s8[4194304]{0:T(1024)(128)(4,1)S(1)}, s32[]{:S(2)}) async-start(s8[8388608]{0:T(1024)(128)(4,1)} %bitcast.163), calls=%async_computation.15 | async-start | bytes 8388608
  203.8 8.6 %copy-start.25 = (f32[4096,384]{0,1:T(8,128)}, f32[4096,384]{0,1:T(8,128)S(1)}, u32[]{:S(2)}) copy-start(f32[4096,384]{0,1:T(8,128)S(1)} %fusion.67) | copy-start | bytes 18874372
  203.8 11.3 %slice-start.7 = ((s8[8388608]{0:T(1024)(128)(4,1)}), s8[4194304]{0:T(1024)(128)(4,1)S(1)}, s32[]{:S(2)}) async-start(s8[8388608]{0:T(1024)(128)(4,1)} %bitcast.163), calls=%async_computation.16 | async-start | bytes 8388608
  222.7 207.5 %all-gather.17.cloned.1.call-start = ((), (), s32[]{:S(2)}) async-start(), calls=%async_computation.4 | async-start | bytes 7077888 | tf_op jit(solution)/shard_map/all_gather | solution.py:206
  234.9 195.3 %all-gather.19.cloned.1.call-start = ((), (), s32[]{:S(2)}) async-start(), calls=%async_computation.5 | async-start | bytes 7077888 | tf_op jit(solution)/shard_map/all_gather | solution.py:207
  246.5 191.2 %all-gather.25.cloned.1.call-start = ((), (), s32[]{:S(2)}) async-start(), calls=%async_computation.8 | async-start | bytes 9437184 | tf_op jit(solution)/shard_map/all_gather | solution.py:209
  246.7 10.2 %copy-start.6 = (bf16[8,64,1024]{2,1,0:T(8,128)(2,1)S(1)}, bf16[8,64,1024]{2,1,0:T(8,128)(2,1)}, u32[]{:S(2)}) copy-start(bf16[8,64,1024]{2,1,0:T(8,128)(2,1)} %fusion.30) | copy-start | bytes 3145732
  273.2 3.9 copy-start.4
  273.2 47.3 %all-to-all-start = ((bf16[8,8,64,256]{3,2,1,0:T(8,128)(2,1)}), bf16[8,8,64,256]{3,2,1,0:T(8,128)(2,1)S(1)}, u32[]{:S(2)}, u32[]{:S(2)}) async-start(bf16[8,8,64,256]{3,2,1,0:T(8,128)(2,1)} %get-tuple-element.15), calls=%async_computation | async-start | bytes 4194304 | tf_op jit(solution)/shard_map/all_to_all | solution.py:189
  277.1 7.8 %copy-start.24 = (f32[512,3072]{1,0:T(8,128)S(1)}, f32[512,3072]{1,0:T(8,128)}, u32[]{:S(2)}) copy-start(f32[512,3072]{1,0:T(8,128)} %fusion.86) | copy-start | bytes 18874372
  320.5 79.2 %all-to-all-start.1 = ((bf16[8,8,64,512]{3,2,1,0:T(8,128)(2,1)}), bf16[8,8,64,512]{3,2,1,0:T(8,128)(2,1)}, u32[]{:S(2)}, u32[]{:S(2)}) async-start(bf16[8,8,64,512]{3,2,1,0:T(8,128)(2,1)} %get-tuple-element.16), calls=%async_computation.1 | async-start | bytes 8388608 | tf_op jit(solution)/shard_map/all_to_all | solution.py:190
  325.9 10.5 %copy-start.27 = (bf16[512,3072]{1,0:T(8,128)(2,1)S(1)}, bf16[512,3072]{1,0:T(8,128)(2,1)}, u32[]{:S(2)}) copy-start(bf16[512,3072]{1,0:T(8,128)(2,1)} %convolution_convert_fusion.3) | copy-start | bytes 9437188
  336.4 12.5 %copy-start.20 = (f32[8,128]{1,0:T(8,128)S(1)}, f32[8,128]{1,0:T(8,128)}, u32[]{:S(2)}) copy-start(f32[8,128]{1,0:T(8,128)} %get-tuple-element.17) | copy-start | bytes 12292
  336.4 12.5 %copy-start.21 = (bf16[2048,1024]{1,0:T(8,128)(2,1)S(1)}, bf16[2048,1024]{1,0:T(8,128)(2,1)}, u32[]{:S(2)}) copy-start(bf16[2048,1024]{1,0:T(8,128)(2,1)} %param.19) | copy-start | bytes 12582916
  403.0 4.2 copy-start.7
  403.0 4.2 copy-start.8
  403.0 4.2 copy-start.9
  410.3 17.5 %copy-start.10 = (bf16[512,1024]{1,0:T(8,128)(2,1)S(1)}, bf16[512,1024]{1,0:T(8,128)(2,1)}, u32[]{:S(2)}) copy-start(bf16[512,1024]{1,0:T(8,128)(2,1)} %fusion.46) | copy-start | bytes 3145732
  410.4 17.5 %copy-start.11 = (bf16[512,1024]{1,0:T(8,128)(2,1)S(1)}, bf16[512,1024]{1,0:T(8,128)(2,1)}, u32[]{:S(2)}) copy-start(bf16[512,1024]{1,0:T(8,128)(2,1)} %bitcast_convert_fusion.1) | copy-start | bytes 3145732
  437.7 4.6 copy-start.3
  447.9 4.1 slice-start
  449.9 7.0 %slice-start.2 = ((s8[6291456]{0:T(1024)(128)(4,1)}), s8[4194304]{0:T(1024)(128)(4,1)S(1)}, s32[]{:S(2)}) async-start(s8[6291456]{0:T(1024)(128)(4,1)} %bitcast.139), calls=%async_computation.11 | async-start | bytes 8388608
  453.6 7.0 %slice-start.4 = ((s8[6291456]{0:T(1024)(128)(4,1)}), s8[4194304]{0:T(1024)(128)(4,1)S(1)}, s32[]{:S(2)}) async-start(s8[6291456]{0:T(1024)(128)(4,1)} %bitcast.141), calls=%async_computation.13 | async-start | bytes 8388608
  457.5 4.4 slice-start.5
  457.5 7.1 %copy-start.1 = (f32[16,128]{1,0:T(8,128)S(1)}, f32[16,128]{1,0:T(8,128)}, u32[]{:S(2)}) copy-start(f32[16,128]{1,0:T(8,128)} %param.24) | copy-start | bytes 24580
  (13 other events, 37.6 us)
Sparse Core Ops, SparseCore 0:
  9.7 51.0 all-gather.22
  63.0 46.6 all-gather.20
  187.9 28.9 all-gather.12
  222.8 37.6 all-gather.14
  261.9 54.7 all-gather.16
  318.2 70.9 all-gather.18
  391.3 46.2 all-gather.24
